TPU v7x, 32 devices: a whole 2x2x4 slice. The times are simulated.
32 devices in a mesh: sub: 2 (over y), row: 4 (over x, core), col: 4 (over z).
Axes of the slice: x: 2, y: 2, z: 4, core: 2. Of those that a mesh axis runs over, the one named last changes fastest.
Arguments:
- factor_window: bfloat16 [2, 8192, 1024], P('sub', ('row', 'col'))
- right_sides: bfloat16 [2, 8192, 2048], P('sub', 'row', 'col'), may hold values from -1.1953125 to 1.1953125
- first_block: int32 [2, 8], P('sub'), may hold values from 0 to 4
- tile_map: int32 [2, 8], P('sub'), may hold values from 0 to 15, as said below
- interface_block: float32 [4096, 4096], P(('sub', 'row'), 'col'), may hold values from -6 to 6
Outputs:
- updated_sides: bfloat16 [2, 8192, 2048], P('sub', 'row', 'col')
- schur_global: float32 [4096, 4096], P(('sub', 'row'), 'col')
Inputs may be any that keep to these rules, and one draw needn't show every extreme that they name: `tile_map`: the 8 entries of a subdomain are different global tiles.
All inputs are finite; a program needn't handle non-finite values.
Results may differ from a plain program's by a relative error of at most 0.0075.
Values may be sent and summed in bfloat16 or wider, within the bound.
A program may use at most 64 MiB of HBM per device.

v0:
```python
import jax
import jax.numpy as jnp
from jax import lax
from jax.sharding import PartitionSpec as P

PANEL = 256
BLOCK = 256
STEPS = 4
GTILES = 16


def spread_2(value, axis, source):
    kept = jnp.where(lax.axis_index(axis) == source, value, 0).astype(value.dtype)
    return lax.psum(kept, axis)


def spread_tiles(columns, tile_map, block_count):
    onehot = (tile_map[0][:, None] == jnp.arange(GTILES, dtype=jnp.int32)[None, :]).astype(
        jnp.bfloat16
    )
    height = columns.shape[0]
    spread = jnp.einsum(
        "qbj,bg->qgj",
        columns.reshape(height, block_count, BLOCK),
        onehot,
        preferred_element_type=jnp.float32,
    )
    return spread.reshape(height, GTILES * BLOCK).astype(jnp.bfloat16)


def local(factor_window, right_sides, first_block, tile_map, interface_block):
    row_count = lax.axis_size("row")
    row_pos = lax.axis_index("row")
    col_pos = lax.axis_index("col")
    local_factor = factor_window[0]
    local_sides = right_sides[0]
    block_rows = local_sides.shape[0]
    block_cols = local_sides.shape[1]
    block_count = first_block.shape[1]
    row_global = row_pos * block_rows + jnp.arange(block_rows, dtype=jnp.int32)
    col_global = col_pos * block_cols + jnp.arange(block_cols, dtype=jnp.int32)
    col_block = col_global // BLOCK
    block_ids = jnp.arange(block_count, dtype=jnp.int32)
    first_col = jnp.sum(
        jnp.where(col_block[:, None] == block_ids[None, :], first_block[0][None, :], 0), axis=1
    )
    live = (row_global // PANEL)[:, None] >= first_col[None, :]
    current = jnp.where(live, local_sides.astype(jnp.float32), jnp.float32(0.0))
    is_root = row_pos == 0
    factor_rows = lax.all_gather(local_factor, "col", axis=0, tiled=True)
    pieces = []
    for panel in range(STEPS):
        offset = panel * PANEL
        panel_cols = factor_rows[:, offset : offset + PANEL]
        diag_block = panel_cols[offset : offset + PANEL].astype(jnp.float32)
        diag_block = jnp.where(is_root, diag_block, jnp.eye(PANEL, dtype=jnp.float32))
        solved = jax.scipy.linalg.solve_triangular(
            diag_block, current[offset : offset + PANEL], lower=True
        ).astype(jnp.bfloat16)
        solved = spread_2(solved, "row", 0)
        update = jnp.dot(panel_cols, solved, preferred_element_type=jnp.float32)
        current = jnp.where((row_global >= offset + PANEL)[:, None], current - update, current)
        placed = jnp.where(is_root, solved.astype(jnp.float32), current[offset : offset + PANEL])
        current = current.at[offset : offset + PANEL].set(placed)
        pieces.append(solved)
    updated_sides = current.astype(jnp.bfloat16)[None]
    stacked = jnp.concatenate(pieces, axis=0)
    out_cols = interface_block.shape[1]
    share = stacked.shape[0] // row_count
    my_share = lax.dynamic_slice_in_dim(stacked, row_pos * share, share, 0)
    all_columns = lax.all_gather(my_share, "col", axis=1, tiled=True)
    spread = spread_tiles(all_columns, tile_map, block_count)
    my_columns = lax.dynamic_slice_in_dim(spread, col_pos * out_cols, out_cols, 1)
    summed = lax.psum_scatter(
        lax.dot_general(
            spread, my_columns, (((0,), (0,)), ((), ())), preferred_element_type=jnp.float32
        ).astype(jnp.bfloat16),
        ("sub", "row"),
        scatter_dimension=0,
        tiled=True,
    ).astype(jnp.float32)
    schur_global = interface_block - summed
    return (updated_sides, schur_global)


def solution(mesh):
    return jax.shard_map(
        local,
        mesh=mesh,
        in_specs=(
            P("sub", ("row", "col"), None),
            P("sub", "row", "col"),
            P("sub", None),
            P("sub", None),
            P(("sub", "row"), "col"),
        ),
        out_specs=(P("sub", "row", "col"), P(("sub", "row"), "col")),
        check_vma=False,
    )
```

profile of v0, /device:TPU:3, one launch (start us, length us, event | category | flops | bytes accessed | tf_op | source)
XLA Modules:
  0.0 393.1 jit_solution(10873900418680429173)
XLA Ops:
  8.8 3.5 convert_select_fusion
  12.3 79.1 %all-gather.6.cloned.1.call-done = bf16[1,2048,1024]{2,1,0:T(8,128)(2,1)} async-done(((bf16[1,512,1024]{2,1,0:T(8,128)(2,1)}), bf16[1,2048,1024]{2,1,0:T(8,128)(2,1)}) %all-gather.6.cloned.1.call-update) | async-done | bytes 4194320 | tf_op jit(solution)/shard_map/all_gather | solution.py:50
  92.7 3.8 while.12
  96.5 19.7 %custom-call.6 = f32[2,128,128]{1,2,0:T(8,128)S(1)} custom-call(f32[2,128,128]{2,1,0:T(8,128)S(1)} %get-tuple-element.77), custom_call_target="InvertDiagBlocksLowerTriangular" | custom-call | tf_op jit(solution)/shard_map/jit(_solve_triangular)/triangular_solve | solution.py:57
  120.1 4.0 %while.13 = (s32[]{:T(128)}, f32[256,256]{1,0:T(8,128)S(1)}, s32[2,2]{1,0:T(2,128)S(1)}, f32[2,128,128]{2,1,0:T(8,128)S(1)}, s32[]{:T(128)}) while((s32[]{:T(128)}, f32[256,256]{1,0:T(8,128)S(1)}, s32[2,2]{1,0:T(2,128)S(1)}, f32[2,128,128]{2,1,0:T(8,128)S(1)}, s32[]{:T(128)}) %tuple.113), condition=%wide.while_cond.4.clone, body=%wide.while_body.4.clone.sunk | while | flops 2 | bytes 131181 | solution.py:57
  124.2 19.7 %custom-call.7 = f32[2,128,128]{1,2,0:T(8,128)S(1)} custom-call(f32[2,128,128]{2,1,0:T(8,128)S(1)} %get-tuple-element.78), custom_call_target="InvertDiagBlocksLowerTriangular" | custom-call | tf_op jit(solution)/shard_map/jit(_solve_triangular)/triangular_solve | solution.py:57
  143.8 5.7 %all-reduce.5.cloned.1.call-done = bf16[256,512]{1,0:T(8,128)(2,1)} async-done(((bf16[256,512]{1,0:T(8,128)(2,1)}), bf16[256,512]{1,0:T(8,128)(2,1)}) %all-reduce.5.cloned.1.call-update) | async-done | bytes 262160 | tf_op jit(solution)/shard_map/psum | solution.py:14
  149.6 3.4 subtract_select_fusion.3
  156.9 4.0 %while.14 = (s32[]{:T(128)}, f32[256,256]{1,0:T(8,128)S(1)}, s32[2,2]{1,0:T(2,128)S(1)}, f32[2,128,128]{2,1,0:T(8,128)S(1)}, s32[]{:T(128)}) while((s32[]{:T(128)}, f32[256,256]{1,0:T(8,128)S(1)}, s32[2,2]{1,0:T(2,128)S(1)}, f32[2,128,128]{2,1,0:T(8,128)S(1)}, s32[]{:T(128)}) %tuple.114), condition=%wide.while_cond.4.clone.1, body=%wide.while_body.4.clone.1.sunk | while | flops 2 | bytes 131181 | solution.py:57
  160.9 19.7 %custom-call.8 = f32[2,128,128]{1,2,0:T(8,128)S(1)} custom-call(f32[2,128,128]{2,1,0:T(8,128)S(1)} %get-tuple-element.79), custom_call_target="InvertDiagBlocksLowerTriangular" | custom-call | tf_op jit(solution)/shard_map/jit(_solve_triangular)/triangular_solve | solution.py:57
  180.6 8.8 %all-reduce.7.cloned.1.call-done = bf16[256,512]{1,0:T(8,128)(2,1)} async-done(((bf16[256,512]{1,0:T(8,128)(2,1)}), bf16[256,512]{1,0:T(8,128)(2,1)}) %all-reduce.7.cloned.1.call-update) | async-done | bytes 262160 | tf_op jit(solution)/shard_map/psum | solution.py:14
  189.5 3.4 subtract_select_fusion.2
  193.4 1.6 copy-done.1
  196.6 3.8 while.15
  200.4 19.7 %custom-call.9 = f32[2,128,128]{1,2,0:T(8,128)S(1)} custom-call(f32[2,128,128]{2,1,0:T(8,128)S(1)} %get-tuple-element.80), custom_call_target="InvertDiagBlocksLowerTriangular" | custom-call | tf_op jit(solution)/shard_map/jit(_solve_triangular)/triangular_solve | solution.py:57
  220.1 9.2 %all-reduce.9.cloned.1.call-done = bf16[256,512]{1,0:T(8,128)(2,1)} async-done(((bf16[256,512]{1,0:T(8,128)(2,1)}), bf16[256,512]{1,0:T(8,128)(2,1)}) %all-reduce.9.cloned.1.call-update) | async-done | bytes 262160 | tf_op jit(solution)/shard_map/psum | solution.py:14
  229.3 3.4 subtract_select_fusion.1
  236.4 32.3 %all-reduce.11.cloned.1.call-done = bf16[256,512]{1,0:T(8,128)(2,1)} async-done(((bf16[256,512]{1,0:T(8,128)(2,1)}), bf16[256,512]{1,0:T(8,128)(2,1)}) %all-reduce.11.cloned.1.call-update) | async-done | bytes 262160 | tf_op jit(solution)/shard_map/psum | solution.py:14
  268.7 3.4 subtract_select_fusion
  272.1 1.6 fusion.19
  274.0 29.2 %all-gather.4.cloned.1.call-done = bf16[256,2048]{1,0:T(8,128)(2,1)} async-done(((bf16[256,512]{1,0:T(8,128)(2,1)}), bf16[256,2048]{1,0:T(8,128)(2,1)}) %all-gather.4.cloned.1.call-update) | async-done | bytes 1048592 | tf_op jit(solution)/shard_map/all_gather | solution.py:71
  306.5 5.6 %convolution_convert_fusion = bf16[4096,1024]{1,0:T(8,128)(2,1)} fusion(bf16[256,4096]{1,0:T(8,128)(2,1)S(1)} %bitcast.105, s32[]{:T(128)S(6)} %select_n.126), kind=kOutput, calls=%fused_computation.8 | convolution fusion | flops 2151677952 | bytes 11010052 | tf_op jit(solution)/shard_map/dot_general | solution.py:75
  312.1 71.3 %reduce-scatter.2.cloned.1.call-done = bf16[512,1024]{1,0:T(8,128)(2,1)} async-done(((bf16[4096,1024]{1,0:T(8,128)(2,1)}), bf16[512,1024]{1,0:T(8,128)(2,1)}) %reduce-scatter.2.cloned.1.call-update) | async-done | bytes 1048592 | tf_op jit(solution)/shard_map/reduce_scatter | solution.py:74
  383.5 2.8 convert_subtract_fusion
  (95 shorter events, 35.5 us)
Async XLA Ops:
  7.2 84.2 %all-gather.6.cloned.1.call-start = ((), (), s32[]{:S(2)}) async-start(), calls=%async_computation.7 | async-start | bytes 5242880 | tf_op jit(solution)/shard_map/all_gather | solution.py:50
  7.9 141.7 %all-reduce.5.cloned.1.call-start = ((), (), s32[]{:S(2)}) async-start(), calls=%async_computation.1 | async-start | bytes 524288 | tf_op jit(solution)/shard_map/psum | solution.py:14
  12.3 137.3 %copy-start.6 = (bf16[1,2048,512]{2,1,0:T(8,128)(2,1)S(1)}, bf16[1,2048,512]{2,1,0:T(8,128)(2,1)}, u32[]{:S(2)}) copy-start(bf16[1,2048,512]{2,1,0:T(8,128)(2,1)} %param.16) | copy-start | bytes 6291460
  120.0 69.4 %all-reduce.7.cloned.1.call-start = ((), (), s32[]{:S(2)}) async-start(), calls=%async_computation.2 | async-start | bytes 524288 | tf_op jit(solution)/shard_map/psum | solution.py:14
  149.6 3.4 copy-start.8
  153.1 2.0 copy-start.2
  156.7 72.6 %all-reduce.9.cloned.1.call-start = ((), (), s32[]{:S(2)}) async-start(), calls=%async_computation.3 | async-start | bytes 524288 | tf_op jit(solution)/shard_map/psum | solution.py:14
  189.5 3.4 copy-start.4
  193.0 2.0 copy-start.1
  196.5 72.2 %all-reduce.11.cloned.1.call-start = ((), (), s32[]{:S(2)}) async-start(), calls=%async_computation.4 | async-start | bytes 524288 | tf_op jit(solution)/shard_map/psum | solution.py:14
  229.3 3.4 copy-start.5
  232.8 2.0 copy-start
  236.3 66.8 %all-gather.4.cloned.1.call-start = ((), (), s32[]{:S(2)}) async-start(), calls=%async_computation.5 | async-start | bytes 1310720 | tf_op jit(solution)/shard_map/all_gather | solution.py:71
  236.4 68.3 %copy-start.10 = (s32[1,8]{1,0:T(1,128)S(1)}, s32[1,8]{1,0:T(1,128)}, u32[]{:S(2)}) copy-start(s32[1,8]{1,0:T(1,128)} %param.18) | copy-start | bytes 100
  268.7 3.4 copy-start.9
  273.7 32.8 %copy-start.3 = (bf16[2048,512]{1,0:T(8,128)(2,1)}, bf16[2048,512]{1,0:T(8,128)(2,1)S(1)}, u32[]{:S(2)}) copy-start(bf16[2048,512]{1,0:T(8,128)(2,1)S(1)} %get-tuple-element.126) | copy-start | bytes 6291460
  273.7 109.7 %reduce-scatter.2.cloned.1.call-start = ((), (), s32[]{:S(2)}) async-start(), calls=%async_computation.6 | async-start | bytes 9437184 | tf_op jit(solution)/shard_map/reduce_scatter | solution.py:74
  312.1 71.4 %copy-start.7 = (f32[512,1024]{1,0:T(8,128)S(1)}, f32[512,1024]{1,0:T(8,128)}, u32[]{:S(2)}) copy-start(f32[512,1024]{1,0:T(8,128)} %param.19) | copy-start | bytes 6291460
Sparse Core Ops, SparseCore 0:
  9.5 81.8 all-gather.5
  120.2 29.3 all-reduce.4
  156.8 32.5 all-reduce.6
  196.7 32.5 all-reduce.8
  236.5 32.2 all-reduce.10
  273.8 29.2 all-gather.3
  312.2 71.1 reduce-scatter.1
where the time goes:
time: 395 us; the launch traced here: 393 us
  waiting for transfers between devices  236 us (60%)
  other arithmetic  92 us (23%)
  matrix products  26.7 us (7%)
  local copies, waits for them, and re-layouts  22.7 us (6%)
  between operations  14.5 us (4%)
    another operation x6, other arithmetic, local(): jax.scipy.linalg.solve_triangular(diag_block, current[offset:offset + PAN...  79.9 us
    all_gather x1, waiting for transfers between devices, local(): factor_rows = lax.all_gather(local_factor, 'col', axis=0, tiled=True)  79.1 us
    reduce_scatter x1, waiting for transfers between devices, local(): lax.psum_scatter(lax.dot_general(spread, my_columns, (((0,), (0,)), ((),...  71.3 us
    psum x4, waiting for transfers between devices, spread_2(): return lax.psum(kept, axis)  56.1 us
    all_gather x1, waiting for transfers between devices, local(): all_columns = lax.all_gather(my_share, 'col', axis=1, tiled=True)  29.2 us
    another operation x29, local copies, waits for them, and re-layouts, local(): jax.scipy.linalg.solve_triangular(diag_block, current[offset:offset + PAN...  15.5 us
    dot_general x4, matrix products, local(): update = jnp.dot(panel_cols, solved, preferred_element_type=jnp.float32)  13.4 us
  transfers between devices with their start and end apart: 7, of which 7 were waited for; matrix products, arithmetic and copies ran while one was open for 19% of the time, Pallas kernels for 0%

commit v1 on v0

v1 whole, which is shorter than its diff:
```python
import functools
import math

import jax
import jax.numpy as jnp
from jax import lax
from jax.experimental import pallas as pl
from jax.experimental.pallas import tpu as pltpu
from jax.sharding import PartitionSpec as P

PANEL = 256
BLOCK = 256
STEPS = 4
GTILES = 16
TINY = 16
EXACT = lax.Precision.HIGHEST


def iota(shape, dim):
    return lax.broadcasted_iota(jnp.int32, shape, dim)


def invert(diag):
    n = diag.shape[0]
    rows, cols = iota((n, n), 0), iota((n, n), 1)
    lower = jnp.where(rows >= cols, diag.astype(jnp.float32), 0.0)
    same = (rows >> 4) == (cols >> 4)
    fold = jnp.where((iota((n, 128), 0) & (TINY - 1)) == iota((n, 128), 1), 1.0, 0.0)
    compact = jnp.dot(
        jnp.where(same, lower, 0.0).astype(jnp.bfloat16),
        fold.astype(jnp.bfloat16),
        preferred_element_type=jnp.float32,
    )
    a = compact.reshape(n // TINY, TINY, 128)
    y = fold.reshape(n // TINY, TINY, 128)
    place = iota(y.shape, 1)
    for j in range(TINY):
        pivot = y[:, j : j + 1, :] / a[:, j : j + 1, j : j + 1]
        y = jnp.where(place == j, pivot, jnp.where(place > j, y - a[:, :, j : j + 1] * pivot, y))
    full = lax.dot_general(
        y.reshape(n, 128),
        fold,
        (((1,), (1,)), ((), ())),
        precision=EXACT,
        preferred_element_type=jnp.float32,
    )
    inverse = jnp.where(same, full, 0.0)
    level = 4
    while (1 << level) < n:
        off = ((rows >> (level + 1)) == (cols >> (level + 1))) & ((rows >> level) != (cols >> level))
        inner = jnp.dot(
            jnp.where(off, lower, 0.0), inverse, precision=EXACT, preferred_element_type=jnp.float32
        )
        inverse = inverse - jnp.dot(
            inverse, inner, precision=EXACT, preferred_element_type=jnp.float32
        )
        level += 1
    return inverse


def solve_kernel(first_ref, l_ref, r_ref, x_ref):
    for p in range(STEPS):
        at = slice(p * PANEL, (p + 1) * PANEL)
        inverse = invert(l_ref[at, at])
        right = jnp.where(first_ref[...] <= p, r_ref[at, :].astype(jnp.float32), 0.0)
        if p:
            right = right - jnp.dot(
                l_ref[at, : p * PANEL], x_ref[: p * PANEL, :], preferred_element_type=jnp.float32
            )
        x_ref[at, :] = jnp.dot(
            inverse, right, precision=EXACT, preferred_element_type=jnp.float32
        ).astype(jnp.bfloat16)


def solve(first_col, factor_rows, sides):
    window, bc = factor_rows.shape[1], sides.shape[1]
    return pl.pallas_call(
        solve_kernel,
        out_shape=jax.ShapeDtypeStruct((window, bc), jnp.bfloat16),
        grid=(1,),
        in_specs=[
            pl.BlockSpec((1, bc), lambda i: (0, 0)),
            pl.BlockSpec((window, window), lambda i: (0, 0)),
            pl.BlockSpec((window, bc), lambda i: (0, 0)),
        ],
        out_specs=pl.BlockSpec((window, bc), lambda i: (0, 0)),
        compiler_params=pltpu.CompilerParams(vmem_limit_bytes=48 * 1024 * 1024),
        cost_estimate=pl.CostEstimate(flops=10**10, bytes_accessed=4 * 2**20, transcendentals=0),
    )(first_col, factor_rows, sides)


def schur_kernel(ni, ch, row_src, col_src, *refs):
    a_refs, (b_ref, i_ref, o_ref) = refs[:ni], refs[ni:]
    s, j = pl.program_id(0), pl.program_id(1)

    @pl.when((s == 0) & (j == 0))
    def _():
        o_ref[...] = i_ref[...]

    at = pl.ds(pl.multiple_of(j * ch, ch), ch)
    for i in range(ni):

        @pl.when((row_src[s, i] >= 0) & (col_src[s, j] >= 0))
        def _(i=i):
            a = a_refs[i][0, :, 0].reshape(-1, ch)
            b = b_ref[0, :, 0].reshape(-1, ch)
            term = lax.dot_general(
                a, b, (((0,), (0,)), ((), ())), preferred_element_type=jnp.float32
            )
            o_ref[i * ch : (i + 1) * ch, at] -= term


def schur(full, interface, row_src, col_src, ch):
    subs, rows, _, share, bc = full.shape
    out_rows, out_cols = interface.shape
    ni, nj, per = out_rows // ch, out_cols // ch, bc // ch
    block = (1, rows, 1, share, ch)

    def place(src):
        src = jnp.maximum(src, 0)
        return src // per, src % per

    def a_map(i, s, j, rs, cs):
        c, k = place(rs[s, i])
        return (s, 0, c, 0, k)

    def b_map(s, j, rs, cs):
        c, k = place(cs[s, j])
        return (s, 0, c, 0, k)

    whole = pl.BlockSpec((out_rows, out_cols), lambda s, j, rs, cs: (0, 0))
    return pl.pallas_call(
        functools.partial(schur_kernel, ni, ch),
        out_shape=jax.ShapeDtypeStruct((out_rows, out_cols), jnp.float32),
        grid_spec=pltpu.PrefetchScalarGridSpec(
            num_scalar_prefetch=2,
            grid=(subs, nj),
            in_specs=[pl.BlockSpec(block, functools.partial(a_map, i)) for i in range(ni)]
            + [pl.BlockSpec(block, b_map), whole],
            out_specs=whole,
        ),
        compiler_params=pltpu.CompilerParams(vmem_limit_bytes=48 * 1024 * 1024),
        cost_estimate=pl.CostEstimate(flops=4 * 10**9, bytes_accessed=10 * 2**20, transcendentals=0),
    )(row_src, col_src, *([full] * (ni + 1)), interface)


def chunk_sources(tile_maps, ch):
    count = tile_maps.shape[1]
    hit = tile_maps[:, None, :] == jnp.arange(GTILES, dtype=jnp.int32)[None, :, None]
    block = jnp.sum(jnp.where(hit, jnp.arange(count, dtype=jnp.int32) + 1, 0), axis=2) - 1
    parts = BLOCK // ch
    pieces = block[:, :, None] * parts + jnp.arange(parts, dtype=jnp.int32)
    return jnp.where(block[:, :, None] >= 0, pieces, -1).reshape(tile_maps.shape[0], -1)


def local(factor_window, right_sides, first_block, tile_map, interface_block):
    subs, rows, cols = lax.axis_size("sub"), lax.axis_size("row"), lax.axis_size("col")
    sub_pos, row_pos, col_pos = (lax.axis_index(a) for a in ("sub", "row", "col"))
    sides = right_sides[0]
    block_rows, bc = sides.shape
    window = factor_window.shape[2]
    out_rows, out_cols = interface_block.shape
    is_root = row_pos == 0
    tile_maps = lax.all_gather(tile_map, "sub", axis=0, tiled=True)
    ch = math.gcd(math.gcd(BLOCK, bc), math.gcd(out_rows, out_cols))
    src = chunk_sources(tile_maps, ch)
    row_src = lax.dynamic_slice_in_dim(
        src, (sub_pos * rows + row_pos) * (out_rows // ch), out_rows // ch, 1
    )
    col_src = lax.dynamic_slice_in_dim(src, col_pos * (out_cols // ch), out_cols // ch, 1)

    col_block = (col_pos * bc + jnp.arange(bc, dtype=jnp.int32)) // BLOCK
    ids = jnp.arange(first_block.shape[1], dtype=jnp.int32)
    first_col = jnp.sum(
        jnp.where(col_block[:, None] == ids[None, :], first_block[0][None, :], 0), axis=1
    )[None, :]

    factor_rows = lax.all_gather(factor_window[0], "col", axis=0, tiled=True)
    solved = solve(first_col, factor_rows, sides)
    share = window // rows
    mine = solved[:share]
    for r in range(1, rows):
        sent = lax.ppermute(solved[r * share : (r + 1) * share], "row", [(0, r)])
        mine = jnp.where(row_pos == r, sent, mine)
    full = lax.all_gather(mine, ("sub", "row", "col"), axis=0).reshape(
        subs, rows, cols, share, bc
    )
    own = lax.dynamic_slice(
        full, (sub_pos, 0, col_pos, 0, 0), (1, rows, 1, share, bc)
    ).reshape(window, bc)
    update = jnp.dot(factor_rows, own, preferred_element_type=jnp.float32)
    below = (sides.astype(jnp.float32) - update).astype(jnp.bfloat16)
    in_window = is_root & (jnp.arange(block_rows, dtype=jnp.int32) < window)
    padded = jnp.pad(own, ((0, block_rows - window), (0, 0)))
    updated = jnp.where(in_window[:, None], padded, below)[None]
    return (updated, schur(full, interface_block, row_src, col_src, ch))


def solution(mesh):
    return jax.shard_map(
        local,
        mesh=mesh,
        in_specs=(
            P("sub", ("row", "col"), None),
            P("sub", "row", "col"),
            P("sub", None),
            P("sub", None),
            P(("sub", "row"), "col"),
        ),
        out_specs=(P("sub", "row", "col"), P(("sub", "row"), "col")),
        check_vma=False,
    )
```

time: 395 us -> 231 us (0.58)
  other arithmetic: 92 us -> 1.62 us
  waiting for transfers between devices: 236 us -> 164 us
  Pallas kernels: 0 us -> 33.5 us
  matrix products: 26.7 us -> 3.87 us
  local copies, waits for them, and re-layouts: 22.7 us -> 3.94 us
    another operation x6 -> x0, other arithmetic: 79.9 us -> none  [local(): jax.scipy.linalg.solve_triangular(diag_block, current[offset:offset + PAN...]
    reduce_scatter x1 -> x0, waiting for transfers between devices: 71.3 us -> none  [local(): lax.psum_scatter(lax.dot_general(spread, my_columns, (((0,), (0,)), ((),...]
    psum x4 -> x0, waiting for transfers between devices: 56.1 us -> none  [spread_2(): return lax.psum(kept, axis)]
    all_gather x2, waiting for transfers between devices: 108 us -> 159 us  [the longest x1 82.7 us: local(): factor_rows = lax.all_gather(factor_window[0], 'col', axis=0, tiled=True)]
    pallas_call x0 -> x2, Pallas kernels: none -> 33.5 us  [the longest x1 25.7 us: solve(): pl.pallas_call(solve_kernel, out_shape=jax.ShapeDtypeStruct((window, bc),...]
    dot_general x6 -> x1, matrix products: 19.9 us -> 3.87 us  [local(): update = jnp.dot(factor_rows, own, preferred_element_type=jnp.float32)]
    another operation x29 -> x0, local copies, waits for them, and re-layouts: 15.5 us -> none  [local(): jax.scipy.linalg.solve_triangular(diag_block, current[offset:offset + PAN...]
    another operation x12 -> x0, matrix products: 6.75 us -> none  [local(): jax.scipy.linalg.solve_triangular(diag_block, current[offset:offset + PAN...]
  transfers between devices with their start and end apart: 7 -> 5, of which waited for: 7 -> 3; matrix products, arithmetic and copies ran while one was open for 19% -> 0% of each run, Pallas kernels for 0% -> 0%
where the time goes in v1:
time: 231 us; the launch traced here: 228 us
  waiting for transfers between devices  164 us (71%)
  Pallas kernels  33.5 us (15%)
  between operations  14.1 us (6%)
  starting transfers between devices  4.22 us (2%)
  local copies, waits for them, and re-layouts  3.94 us (2%)
  matrix products  3.87 us (2%)
  blocking collectives  3.08 us (1%)
    all_gather x1, waiting for transfers between devices, local(): factor_rows = lax.all_gather(factor_window[0], 'col', axis=0, tiled=True)  82.7 us
    all_gather x1, waiting for transfers between devices, local(): lax.all_gather(mine, ('sub', 'row', 'col'), axis=0)  76.8 us
    pallas_call x1, Pallas kernels, solve(): pl.pallas_call(solve_kernel, out_shape=jax.ShapeDtypeStruct((window, bc),...  25.7 us
    pallas_call x1, Pallas kernels, schur(): pl.pallas_call(functools.partial(schur_kernel, ni, ch), out_shape=jax.Sha...  7.75 us
  transfers between devices with their start and end apart: 5, of which 3 were waited for; matrix products, arithmetic and copies ran while one was open for 0% of the time, Pallas kernels for 0%

profile of v1, /device:TPU:3, one launch (start us, length us, event | category | flops | bytes accessed | tf_op | source)
XLA Modules:
  0.0 228.4 jit_solution(10376608483432375493)
XLA Ops:
  7.2 0.0 all-gather.6.cloned.1.call-start
  7.2 0.7 all-gather.6.cloned.1.call-update
  7.9 0.0 all-gather.8.cloned.1.call-start
  8.0 0.7 select_reduce_fusion
  8.7 82.7 %all-gather.6.cloned.1.call-done = bf16[1,2048,1024]{2,1,0:T(8,128)(2,1)} async-done(((bf16[1,512,1024]{2,1,0:T(8,128)(2,1)}), bf16[1,2048,1024]{2,1,0:T(8,128)(2,1)}) %all-gather.6.cloned.1.call-update) | async-done | bytes 4194320 | tf_op jit(solution)/shard_map/all_gather | solution.py:178
  91.4 1.6 copy-done.1
  93.0 25.7 %shard_map.68 = bf16[1024,512]{1,0:T(8,128)(2,1)S(1)} custom-call(s32[1,512]{1,0:T(1,128)S(1)} %bitcast.28, bf16[2048,1024]{1,0:T(8,128)(2,1)} %bitcast.37, bf16[2048,512]{1,0:T(8,128)(2,1)S(1)} %bitcast.29), custom_call_target="tpu_custom_call" | custom-call | flops 10000000000 | bytes 4194304 | tf_op jit(solution)/shard_map/pallas_call | solution.py:77
  118.7 0.0 copy-start
  118.7 0.9 fusion.10
  119.6 1.4 collective-permute-start
  121.1 1.4 collective-permute-start.1
  122.4 1.4 collective-permute-start.2
  123.8 3.9 %collective-permute-done = bf16[256,512]{1,0:T(8,128)(2,1)S(1)} collective-permute-done((bf16[256,512]{1,0:T(8,128)(2,1)}, bf16[256,512]{1,0:T(8,128)(2,1)S(1)}, u32[]{:S(2)}, u32[]{:S(2)}) %collective-permute-start) | collective-permute-done | bytes 262176 | tf_op jit(solution)/shard_map/ppermute | solution.py:183
  127.7 0.8 fusion.4
  128.4 0.0 all-gather.8.cloned.1.call-update
  128.5 3.1 %all-gather.2 = s32[2,1,8]{2,1,0:T(1,128)S(1)} all-gather(s32[1,1,8]{2,1,0:T(1,128)S(1)} %bitcast.38), channel_id=1, replica_groups=mesh['sub'=2,'row'=4,'col'=4] {'sub'}, dimensions={0}, use_global_device_ids=true | all-gather | bytes 96 | tf_op jit(solution)/shard_map/all_gather | solution.py:164
  131.5 0.1 select_reduce_fusion.1
  131.6 0.1 dynamic-slice_bitcast_fusion.1.row_src
  131.7 0.1 dynamic-slice_bitcast_fusion.col_src
  131.8 76.8 %all-gather.8.cloned.1.call-done = bf16[8192,512]{1,0:T(8,128)(2,1)} async-done(((bf16[256,512]{1,0:T(8,128)(2,1)}), bf16[8192,512]{1,0:T(8,128)(2,1)}) %all-gather.8.cloned.1.call-update) | async-done | bytes 8388624 | tf_op jit(solution)/shard_map/all_gather | solution.py:185
  208.6 1.3 constant_dynamic-slice_fusion
  209.9 0.0 copy-start.2
  209.9 7.7 %shard_map.69 = f32[512,1024]{1,0:T(8,128)} custom-call(s32[2,2]{1,0:T(2,128)S(1)} %dynamic-slice_bitcast_fusion.1.row_src, s32[2,4]{1,0:T(2,128)S(1)} %dynamic-slice_bitcast_fusion.col_src, bf16[2,4,4,256,512]{4,3,2,1,0:T(8,128)(2,1)} %bitcast.31, bf16[2,4,4,256,512]{4,3,2,1,0:T(8,128)(2,1)} %bitcast.32, bf16[2,4,4,256,512]{4,3,2,1,0:T(8,128)(2,1)} %bitcast.33, ...), custom_call_target="tpu_custom_call" | custom-call | flops 4000000000 | bytes 10485760 | tf_op jit(solution)/shard_map/pallas_call | solution.py:132
  217.7 3.9 %fusion.2 = bf16[1,2048,512]{2,1,0:T(8,128)(2,1)} fusion(bf16[1024,512]{1,0:T(8,128)(2,1)S(1)} %bitcast.34, pred[2048]{0:T(1024)(128)(4,1)S(1)} %fusion.5, bf16[1,2048,512]{2,1,0:T(8,128)(2,1)S(1)} %copy-done.2, bf16[1,2048,1024]{2,1,0:T(8,128)(2,1)S(1)} %copy-done.3), kind=kOutput, calls=%fused_computation.3 | convolution fusion | flops 2151677952 | bytes 9439232 | tf_op jit(solution)/shard_map/dot_general | solution.py:191
  (13 shorter events, 0.0 us)
Async XLA Ops:
  7.2 84.2 %all-gather.6.cloned.1.call-start = ((), (), s32[]{:S(2)}) async-start(), calls=%async_computation | async-start | bytes 5242880 | tf_op jit(solution)/shard_map/all_gather | solution.py:178
  7.9 200.7 %all-gather.8.cloned.1.call-start = ((), (), s32[]{:S(2)}) async-start(), calls=%async_computation.1 | async-start | bytes 8650752 | tf_op jit(solution)/shard_map/all_gather | solution.py:185
  91.4 1.6 copy-start.1
  93.0 35.5 %copy-start.4 = (s32[1,8]{1,0:T(1,128)S(1)}, s32[1,8]{1,0:T(1,128)}, u32[]{:S(2)}) copy-start(s32[1,8]{1,0:T(1,128)} %param.8) | copy-start | bytes 100
  118.7 91.2 %copy-start = (f32[512,1024]{1,0:T(8,128)S(1)}, f32[512,1024]{1,0:T(8,128)}, u32[]{:S(2)}) copy-start(f32[512,1024]{1,0:T(8,128)} %refs_3_.1) | copy-start | bytes 6291460
  119.6 8.0 %collective-permute-start = (bf16[256,512]{1,0:T(8,128)(2,1)}, bf16[256,512]{1,0:T(8,128)(2,1)S(1)}, u32[]{:S(2)}, u32[]{:S(2)}) collective-permute-start(bf16[256,512]{1,0:T(8,128)(2,1)} %get-tuple-element.4), channel_id=1, source_target_pairs={{0,12},{1,13},{2,14},{3,15},{16,28},{17,29},{18,30},{19,31}} | collective-permute-start | bytes 786440 | tf_op jit(solution)/shard_map/ppermute | solution.py:183
  121.1 6.6 %collective-permute-start.1 = (bf16[256,512]{1,0:T(8,128)(2,1)}, bf16[256,512]{1,0:T(8,128)(2,1)}, u32[]{:S(2)}, u32[]{:S(2)}) collective-permute-start(bf16[256,512]{1,0:T(8,128)(2,1)} %get-tuple-element.3), channel_id=1, source_target_pairs={{0,8},{1,9},{2,10},{3,11},{16,24},{17,25},{18,26},{19,27}} | collective-permute-start | bytes 786440 | tf_op jit(solution)/shard_map/ppermute | solution.py:183
  122.4 5.2 %collective-permute-start.2 = (bf16[256,512]{1,0:T(8,128)(2,1)}, bf16[256,512]{1,0:T(8,128)(2,1)}, u32[]{:S(2)}, u32[]{:S(2)}) collective-permute-start(bf16[256,512]{1,0:T(8,128)(2,1)} %get-tuple-element.2), channel_id=1, source_target_pairs={{0,4},{1,5},{2,6},{3,7},{16,20},{17,21},{18,22},{19,23}} | collective-permute-start | bytes 786440 | tf_op jit(solution)/shard_map/ppermute | solution.py:183
  209.9 7.8 %copy-start.2 = (bf16[1,2048,512]{2,1,0:T(8,128)(2,1)S(1)}, bf16[1,2048,512]{2,1,0:T(8,128)(2,1)}, u32[]{:S(2)}) copy-start(bf16[1,2048,512]{2,1,0:T(8,128)(2,1)} %param.6) | copy-start | bytes 6291460
  209.9 7.8 %copy-start.3 = (bf16[1,2048,1024]{2,1,0:T(8,128)(2,1)S(1)}, bf16[1,2048,1024]{2,1,0:T(8,128)(2,1)}, u32[]{:S(2)}) copy-start(bf16[1,2048,1024]{2,1,0:T(8,128)(2,1)} %all-gather.6.cloned.1.call-done) | copy-start | bytes 12582916
Sparse Core Ops, SparseCore 0:
  9.5 81.8 all-gather.5
  128.6 79.9 all-gather.7

commit v2 on v1

--- a/solution.py
+++ b/solution.py
@@ -175,8 +175,28 @@
         jnp.where(col_block[:, None] == ids[None, :], first_block[0][None, :], 0), axis=1
     )[None, :]
 
-    factor_rows = lax.all_gather(factor_window[0], "col", axis=0, tiled=True)
-    solved = solve(first_col, factor_rows, sides)
+    factor = factor_window[0]
+    height = factor.shape[0]
+    holders = window // height
+    early = [factor] + [
+        lax.ppermute(factor, ("row", "col"), [(h, (h + k) % cols) for h in range(holders)])
+        for k in range(1, cols)
+    ]
+    pieces = []
+    for h in range(holders):
+        piece = factor
+        for k in range(1, cols):
+            piece = jnp.where((col_pos - h + cols) % cols == k, early[k], piece)
+        pieces.append(piece)
+    window_rows = jnp.concatenate(pieces, axis=0)
+    factor, window_rows = lax.optimization_barrier((factor, window_rows))
+    solved = solve(first_col, window_rows, sides)
+    factor_rows = jnp.zeros((cols * height, window), factor.dtype)
+    for k in range(cols):
+        ring = [(c, (c + k) % cols) for c in range(cols)]
+        piece = lax.ppermute(factor, "col", ring) if k else factor
+        start = ((col_pos - k + cols) % cols) * height
+        factor_rows = lax.dynamic_update_slice(factor_rows, piece, (start, 0))
     share = window // rows
     mine = solved[:share]
     for r in range(1, rows):

time: 231 us -> 252 us (1.091)
  starting transfers between devices: 4.22 us -> 20.4 us
  local copies, waits for them, and re-layouts: 3.94 us -> 10.3 us
    all_gather x1 -> x0, waiting for transfers between devices: 82.7 us -> none  [local(): factor_rows = lax.all_gather(factor_window[0], 'col', axis=0, tiled=True)]
    ppermute x0 -> x6, waiting for transfers between devices: none -> 71.9 us  [the longest x3 71.9 us: local(): piece = lax.ppermute(factor, 'col', ring) if k else factor]
    ppermute x3, waiting for transfers between devices: 3.87 us -> 43 us  [local(): sent = lax.ppermute(solved[r * share:(r + 1) * share], 'row', [(0, r)])]
    all_gather x1, waiting for transfers between devices: 76.8 us -> 46.9 us  [local(): lax.all_gather(mine, ('sub', 'row', 'col'), axis=0)]
    ppermute x0 -> x6, starting transfers between devices: none -> 17.7 us  [the longest x3 15.5 us: local(): piece = lax.ppermute(factor, 'col', ring) if k else factor]
    dynamic_update_slice x0 -> x4, local copies, waits for them, and re-layouts: none -> 5.53 us  [local(): factor_rows = lax.dynamic_update_slice(factor_rows, piece, (start, 0))]
  transfers between devices with their start and end apart: 5 -> 10, of which waited for: 3 -> 4; matrix products, arithmetic and copies ran while one was open for 0% -> 4% of each run, Pallas kernels for 0% -> 0%
where the time goes in v2:
time: 252 us; the launch traced here: 251 us
  waiting for transfers between devices  162 us (64%)
  Pallas kernels  31.7 us (13%)
  starting transfers between devices  20.4 us (8%)
  between operations  14.2 us (6%)
  local copies, waits for them, and re-layouts  10.3 us (4%)
  matrix products  6.08 us (2%)
  blocking collectives  3.47 us (1%)
  other arithmetic  3.4 us (1%)
    ppermute x3, waiting for transfers between devices, local(): piece = lax.ppermute(factor, 'col', ring) if k else factor  71.9 us
    all_gather x1, waiting for transfers between devices, local(): lax.all_gather(mine, ('sub', 'row', 'col'), axis=0)  46.9 us
    ppermute x3, waiting for transfers between devices, local(): sent = lax.ppermute(solved[r * share:(r + 1) * share], 'row', [(0, r)])  43 us
    pallas_call x1, Pallas kernels, solve(): pl.pallas_call(solve_kernel, out_shape=jax.ShapeDtypeStruct((window, bc),...  24.2 us
    ppermute x3, starting transfers between devices, local(): piece = lax.ppermute(factor, 'col', ring) if k else factor  15.5 us
    pallas_call x1, Pallas kernels, schur(): pl.pallas_call(functools.partial(schur_kernel, ni, ch), out_shape=jax.Sha...  7.57 us
    dot_general x1, matrix products, local(): update = jnp.dot(factor_rows, own, preferred_element_type=jnp.float32)  6.08 us
    dynamic_update_slice x4, local copies, waits for them, and re-layouts, local(): factor_rows = lax.dynamic_update_slice(factor_rows, piece, (start, 0))  5.53 us
  transfers between devices with their start and end apart: 10, of which 4 were waited for; matrix products, arithmetic and copies ran while one was open for 4% of the time, Pallas kernels for 0%

profile of v2, /device:TPU:3, one launch (start us, length us, event | category | flops | bytes accessed | tf_op | source)
XLA Modules:
  0.0 251.5 jit_solution(1143575938652505898)
XLA Ops:
  7.2 0.7 collective-permute-start.2
  7.9 0.7 collective-permute-start.1
  8.7 0.7 collective-permute-start
  9.5 0.7 select_reduce_fusion
  10.2 1.6 select_select_fusion.1
  12.1 24.2 %shard_map.68 = bf16[1024,512]{1,0:T(8,128)(2,1)S(1)} custom-call(s32[1,512]{1,0:T(1,128)S(1)} %bitcast.21, bf16[1024,1024]{1,0:T(8,128)(2,1)S(1)} %pad_maximum_fusion.l_ref, bf16[2048,512]{1,0:T(8,128)(2,1)S(1)} %bitcast.22), custom_call_target="tpu_custom_call" | custom-call | flops 10000000000 | bytes 4194304 | tf_op jit(solution)/shard_map/pallas_call | solution.py:77
  36.3 0.8 fusion.10
  38.4 1.3 collective-permute-start.3
  39.7 43.0 %collective-permute-done.3 = bf16[256,512]{1,0:T(8,128)(2,1)S(1)} collective-permute-done((bf16[256,512]{1,0:T(8,128)(2,1)S(1)}, bf16[256,512]{1,0:T(8,128)(2,1)S(1)}, u32[]{:S(2)}, u32[]{:S(2)}) %collective-permute-start.3) | collective-permute-done | bytes 262176 | tf_op jit(solution)/shard_map/ppermute | solution.py:203
  82.7 0.8 fusion.3
  83.5 12.5 %collective-permute-start.6 = (bf16[512,1024]{1,0:T(8,128)(2,1)S(1)}, bf16[512,1024]{1,0:T(8,128)(2,1)}, u32[]{:S(2)}, u32[]{:S(2)}) collective-permute-start(bf16[512,1024]{1,0:T(8,128)(2,1)S(1)} %bitcast.30), channel_id=1, source_target_pairs={{0,1},{1,2},{2,3},{3,0},{4,5},{5,6},{6,7},{7,4},{8,9},{9,10},{10,1... | collective-permute-start | bytes 3145736 | tf_op jit(solution)/shard_map/ppermute | solution.py:197
  96.0 3.5 %all-gather.1 = s32[2,1,8]{2,1,0:T(1,128)S(1)} all-gather(s32[1,1,8]{2,1,0:T(1,128)S(1)} %bitcast.37), channel_id=1, replica_groups=mesh['sub'=2,'row'=4,'col'=4] {'sub'}, dimensions={0}, use_global_device_ids=true | all-gather | bytes 96 | tf_op jit(solution)/shard_map/all_gather | solution.py:164
  99.5 3.0 %collective-permute-start.7 = (bf16[512,1024]{1,0:T(8,128)(2,1)S(1)}, bf16[512,1024]{1,0:T(8,128)(2,1)S(1)}, u32[]{:S(2)}, u32[]{:S(2)}) collective-permute-start(bf16[512,1024]{1,0:T(8,128)(2,1)S(1)} %bitcast.31), channel_id=1, source_target_pairs={{0,2},{1,3},{2,0},{3,1},{4,6},{5,7},{6,4},{7,5},{8,10},{9,11},{10,... | collective-permute-start | bytes 3145736 | tf_op jit(solution)/shard_map/ppermute | solution.py:197
  102.8 2.5 broadcast_in_dim.53
  105.3 1.1 constant_dynamic-update-slice_fusion.3
  106.4 21.6 %collective-permute-done.6 = bf16[512,1024]{1,0:T(8,128)(2,1)} collective-permute-done((bf16[512,1024]{1,0:T(8,128)(2,1)S(1)}, bf16[512,1024]{1,0:T(8,128)(2,1)}, u32[]{:S(2)}, u32[]{:S(2)}) %collective-permute-start.6) | collective-permute-done | bytes 1048608 | tf_op jit(solution)/shard_map/ppermute | solution.py:197
  128.0 2.3 constant_dynamic-update-slice_fusion.2
  130.3 50.4 %collective-permute-done.7 = bf16[512,1024]{1,0:T(8,128)(2,1)S(1)} collective-permute-done((bf16[512,1024]{1,0:T(8,128)(2,1)S(1)}, bf16[512,1024]{1,0:T(8,128)(2,1)S(1)}, u32[]{:S(2)}, u32[]{:S(2)}) %collective-permute-start.7) | collective-permute-done | bytes 1048608 | tf_op jit(solution)/shard_map/ppermute | solution.py:197
  180.6 1.1 constant_dynamic-update-slice_fusion.1
  181.7 1.0 constant_dynamic-update-slice_fusion
  182.7 46.9 %all-gather.4.cloned.1.call-done = bf16[8192,512]{1,0:T(8,128)(2,1)} async-done(((bf16[256,512]{1,0:T(8,128)(2,1)}), bf16[8192,512]{1,0:T(8,128)(2,1)}) %all-gather.4.cloned.1.call-update) | async-done | bytes 8388624 | tf_op jit(solution)/shard_map/all_gather | solution.py:205
  229.6 1.3 constant_dynamic-slice_fusion.1
  231.0 7.6 %shard_map.69 = f32[512,1024]{1,0:T(8,128)} custom-call(s32[2,2]{1,0:T(2,128)S(1)} %fusion.9.row_src, s32[2,4]{1,0:T(2,128)S(1)} %fusion.8.col_src, bf16[2,4,4,256,512]{4,3,2,1,0:T(8,128)(2,1)} %bitcast.24, bf16[2,4,4,256,512]{4,3,2,1,0:T(8,128)(2,1)} %bitcast.25, bf16[2,4,4,256,512]{4,3,2,1,0:T(8,128)(2,1)} %bitcast.26, f32[512,1024]{1,0:T(8,128)S(1)} %copy-done), custom_call_target="tpu_custom_call" | custom-call | flops 4000000000 | bytes 10485760 | tf_op jit(solution)/shard_map/pallas_call | solution.py:132
  238.5 6.1 %fusion.1 = bf16[1,2048,512]{2,1,0:T(8,128)(2,1)} fusion(bf16[2048,1024]{1,0:T(8,128)(2,1)} %constant_dynamic-update-slice_fusion, bf16[1024,512]{1,0:T(8,128)(2,1)S(1)} %bitcast.34, pred[2048]{0:T(1024)(128)(4,1)S(1)} %fusion.4, bf16[1,2048,512]{2,1,0:T(8,128)(2,1)S(1)} %copy-done.2), kind=kOutput, calls=%fused_computation.2 | convolution fusion | flops 2151677952 | bytes 9439232 | tf_op jit(solution)/shard_map/dot_general | solution.py:211
  (29 shorter events, 2.0 us)
Async XLA Ops:
  7.2 222.5 %all-gather.4.cloned.1.call-start = ((), (), s32[]{:S(2)}) async-start(), calls=%async_computation | async-start | bytes 8650752 | tf_op jit(solution)/shard_map/all_gather | solution.py:205
  7.2 3.0 %collective-permute-start.2 = (bf16[512,1024]{1,0:T(8,128)(2,1)}, bf16[512,1024]{1,0:T(8,128)(2,1)S(1)}, u32[]{:S(2)}, u32[]{:S(2)}) collective-permute-start(bf16[512,1024]{1,0:T(8,128)(2,1)} %bitcast.27), channel_id=1, source_target_pairs={{0,1},{1,2},{16,17},{17,18}} | collective-permute-start | bytes 3145736 | tf_op jit(solution)/shard_map/ppermute | solution.py:182
  7.9 2.3 collective-permute-start.1
  8.7 1.5 collective-permute-start
  10.2 1.9 copy-start.1
  12.1 71.4 %copy-start.3 = (bf16[1,512,1024]{2,1,0:T(8,128)(2,1)S(1)}, bf16[1,512,1024]{2,1,0:T(8,128)(2,1)}, u32[]{:S(2)}) copy-start(bf16[1,512,1024]{2,1,0:T(8,128)(2,1)} %param.5) | copy-start | bytes 3145732
  12.1 83.9 %copy-start.4 = (s32[1,8]{1,0:T(1,128)S(1)}, s32[1,8]{1,0:T(1,128)}, u32[]{:S(2)}) copy-start(s32[1,8]{1,0:T(1,128)} %param.8) | copy-start | bytes 100
  37.0 2.7 %collective-permute-start.5 = (bf16[256,512]{1,0:T(8,128)(2,1)}, bf16[256,512]{1,0:T(8,128)(2,1)S(1)}, u32[]{:S(2)}, u32[]{:S(2)}) collective-permute-start(bf16[256,512]{1,0:T(8,128)(2,1)} %get-tuple-element.8), channel_id=1, source_target_pairs={{0,4},{1,5},{2,6},{3,7},{16,20},{17,21},{18,22},{19,23}} | collective-permute-start | bytes 786440 | tf_op jit(solution)/shard_map/ppermute | solution.py:203
  37.7 2.0 collective-permute-start.4
  38.4 44.3 %collective-permute-start.3 = (bf16[256,512]{1,0:T(8,128)(2,1)S(1)}, bf16[256,512]{1,0:T(8,128)(2,1)S(1)}, u32[]{:S(2)}, u32[]{:S(2)}) collective-permute-start(bf16[256,512]{1,0:T(8,128)(2,1)S(1)} %get-tuple-element.10), channel_id=1, source_target_pairs={{0,12},{1,13},{2,14},{3,15},{16,28},{17,29},{18,30},{19,31}} | collective-permute-start | bytes 786440 | tf_op jit(solution)/shard_map/ppermute | solution.py:203
  83.5 44.5 %collective-permute-start.6 = (bf16[512,1024]{1,0:T(8,128)(2,1)S(1)}, bf16[512,1024]{1,0:T(8,128)(2,1)}, u32[]{:S(2)}, u32[]{:S(2)}) collective-permute-start(bf16[512,1024]{1,0:T(8,128)(2,1)S(1)} %bitcast.30), channel_id=1, source_target_pairs={{0,1},{1,2},{2,3},{3,0},{4,5},{5,6},{6,7},{7,4},{8,9},{9,10},{10,1... | collective-permute-start | bytes 3145736 | tf_op jit(solution)/shard_map/ppermute | solution.py:197
  99.5 81.1 %collective-permute-start.7 = (bf16[512,1024]{1,0:T(8,128)(2,1)S(1)}, bf16[512,1024]{1,0:T(8,128)(2,1)S(1)}, u32[]{:S(2)}, u32[]{:S(2)}) collective-permute-start(bf16[512,1024]{1,0:T(8,128)(2,1)S(1)} %bitcast.31), channel_id=1, source_target_pairs={{0,2},{1,3},{2,0},{3,1},{4,6},{5,7},{6,4},{7,5},{8,10},{9,11},{10,... | collective-permute-start | bytes 3145736 | tf_op jit(solution)/shard_map/ppermute | solution.py:197
  102.5 79.2 %collective-permute-start.8 = (bf16[512,1024]{1,0:T(8,128)(2,1)S(1)}, bf16[512,1024]{1,0:T(8,128)(2,1)S(1)}, u32[]{:S(2)}, u32[]{:S(2)}) collective-permute-start(bf16[512,1024]{1,0:T(8,128)(2,1)S(1)} %bitcast.32), channel_id=1, source_target_pairs={{0,3},{1,0},{2,1},{3,2},{4,7},{5,4},{6,5},{7,6},{8,11},{9,8},{10,9... | collective-permute-start | bytes 3145736 | tf_op jit(solution)/shard_map/ppermute | solution.py:197
  106.4 124.5 %copy-start = (f32[512,1024]{1,0:T(8,128)S(1)}, f32[512,1024]{1,0:T(8,128)}, u32[]{:S(2)}) copy-start(f32[512,1024]{1,0:T(8,128)} %refs_3_.1) | copy-start | bytes 6291460
  230.9 7.6 %copy-start.2 = (bf16[1,2048,512]{2,1,0:T(8,128)(2,1)S(1)}, bf16[1,2048,512]{2,1,0:T(8,128)(2,1)}, u32[]{:S(2)}) copy-start(bf16[1,2048,512]{2,1,0:T(8,128)(2,1)} %param.6) | copy-start | bytes 6291460
Sparse Core Ops, SparseCore 0:
  83.6 145.9 all-gather.3
